TPU v7x, 256 devices: a 8x8x2 block of a 8x8x16 slice. The times are simulated.
256 devices in a mesh: groups: 2 (over z), ep: 64 (over y, x), tp: 2 (over core).
Axes of the slice: x: 8, y: 8, z: 2, core: 2. Of those that a mesh axis runs over, the one named last changes fastest.
The devices are a block of a 8x8x16 slice.
Arguments:
- hidden: bfloat16 [2048, 3584], P(('groups', 'ep'), 'tp'), parts along dimension 0, may hold values from -6 to 6
- routes: int32 [2048, 8], P(('groups', 'ep')), parts along dimension 0, may hold values from 0 to 63, as said below
- router_weight: bfloat16 [3584, 64], P('tp'), may hold values from -0.1875 to 0.1875
- gate_weight: bfloat16 [64, 3584, 1024], P('ep', None, 'tp'), may hold values from -0.09375 to 0.09375
- up_weight: bfloat16 [64, 3584, 1024], P('ep', None, 'tp'), may hold values from -0.09375 to 0.09375
- down_weight: bfloat16 [64, 1024, 3584], P('ep', 'tp'), may hold values from -0.1875 to 0.1875
- q_latent: bfloat16 [512, 64, 512], P(('groups', 'ep'), 'tp'), parts along dimension 0, may hold values from -48 to 48
- q_rope: bfloat16 [512, 64, 64], P(('groups', 'ep'), 'tp'), parts along dimension 0, may hold values from -48 to 48
- cache_latent: bfloat16 [512, 256, 512], P(('groups', 'ep')), parts along dimension 0, may hold values from -4 to 4
- cache_rope: bfloat16 [512, 64, 256], P(('groups', 'ep')), parts along dimension 0, may hold values from -4 to 4
- lengths: int32 [512], P(('groups', 'ep')), parts along dimension 0, may hold values from 16 to 256, as said below
Outputs:
- moe_out: bfloat16 [2048, 3584], P(('groups', 'ep'), 'tp'), parts along dimension 0
- attn_latent: bfloat16 [512, 64, 512], P(('groups', 'ep'), 'tp'), parts along dimension 0
There are 2 independent parts, one for each index of `groups`. A program takes and returns all parts, laid end to end along the dimension named above; an argument that names none is the same for every part. Nothing has to cross between parts.
Inputs may be any that keep to these rules, and one draw needn't show every extreme that they name: `routes`: each row names 8 different experts; in each aligned block of 16 rows (the rows of one index of ep) no expert is named more than 8 times, and one expert, the same in every block, is named exactly 8 times in each block. `lengths`: one sequence has 256 live positions and one has 16.
All inputs are finite; a program needn't handle non-finite values.
Results may differ from a plain program's by a relative error of at most 0.0085.
Values may be sent and summed in bfloat16 or wider, within the bound.
No kernel may reach another device: no remote copies, remote signals or barrier semaphores. Data moves between devices by JAX's collectives and lax.ppermute only.
A program may use at most 128 MiB of HBM per device.

v0:
```python
import jax
import jax.numpy as jnp
from jax import lax
from jax.sharding import PartitionSpec as P

softmax_scale = 192.0 ** (-0.5)
routed_scale = 2.5


def gathered_total(value, axis):
    tiles = lax.all_gather(value, axis)
    return tiles.sum(axis=0)


def in_blocks(value, dim, devices):
    lengths = value.shape
    tiles = value.reshape(*lengths[:dim], devices, lengths[dim] // devices, *lengths[dim + 1 :])
    return jnp.moveaxis(tiles, dim, 0)


def sum_at_owner(value, axis, dim):
    devices = lax.axis_size(axis)
    tiles = lax.all_to_all(in_blocks(value, dim, devices), axis, 0, 0, tiled=True)
    return jnp.sum(tiles, axis=0)


def local(
    hidden,
    routes,
    router_weight,
    gate_weight,
    up_weight,
    down_weight,
    q_latent,
    q_rope,
    cache_latent,
    cache_rope,
    lengths,
):
    token_count, top_count = routes.shape
    expert_count = lax.axis_size("ep")
    capacity = min(token_count, 4 * token_count * top_count // expert_count)
    partial_logits = jnp.dot(hidden, router_weight, preferred_element_type=jnp.float32)
    logits = gathered_total(partial_logits, "tp")
    affinity = jax.nn.sigmoid(logits)
    expert_iota = jnp.arange(expert_count, dtype=jnp.int32)
    chosen_mask = routes[:, :, None] == expert_iota[None, None, :]
    chosen = jnp.sum(jnp.where(chosen_mask, affinity[:, None, :], 0.0), axis=2)
    gates = routed_scale * chosen / jnp.sum(chosen, axis=1, keepdims=True)
    flat_mask = chosen_mask.reshape(token_count * top_count, expert_count).astype(jnp.int32)
    earlier = jnp.cumsum(flat_mask, axis=0) - flat_mask
    within = jnp.sum(flat_mask * earlier, axis=1).reshape(token_count, top_count)
    slot_index = routes * capacity + within
    slot_iota = jnp.arange(expert_count * capacity, dtype=jnp.int32)
    placing = jnp.sum(
        (slot_index[None, :, :] == slot_iota[:, None, None]).astype(jnp.int32), axis=2
    )
    placing = placing.astype(jnp.bfloat16)
    outgoing = jnp.dot(placing, hidden, preferred_element_type=jnp.float32).astype(jnp.bfloat16)
    outgoing = outgoing.reshape(expert_count, capacity, hidden.shape[1])
    received = lax.all_to_all(outgoing, "ep", split_axis=0, concat_axis=0, tiled=True)
    received = lax.all_gather(received, "tp", axis=2, tiled=True)
    source_count, slot_count, feature_count = received.shape
    flat_rows = received.reshape(source_count * slot_count, feature_count)
    gate_part = jnp.dot(flat_rows, gate_weight[0], preferred_element_type=jnp.float32)
    up_part = jnp.dot(flat_rows, up_weight[0], preferred_element_type=jnp.float32)
    active = (jax.nn.silu(gate_part) * up_part).astype(jnp.bfloat16)
    partial_out = jnp.dot(active, down_weight[0], preferred_element_type=jnp.float32)
    summed = sum_at_owner(partial_out, "tp", 1).astype(jnp.bfloat16)
    summed = summed.reshape(source_count, slot_count, summed.shape[1])
    returned = lax.all_to_all(summed, "ep", split_axis=0, concat_axis=0, tiled=True)
    scores = jnp.einsum("bhl,bjl->bhj", q_latent, cache_latent, preferred_element_type=jnp.float32)
    scores = scores + jnp.einsum(
        "bhr,brj->bhj", q_rope, cache_rope, preferred_element_type=jnp.float32
    )
    scores = scores * softmax_scale
    position = jnp.arange(cache_latent.shape[1], dtype=jnp.int32)
    live = position[None, None, :] < lengths[:, None, None]
    scores = jnp.where(live, scores, -jnp.inf)
    highest = jnp.max(scores, axis=2, keepdims=True)
    expo = jnp.where(live, jnp.exp(scores - highest), 0.0)
    attn_probs = (expo / jnp.sum(expo, axis=2, keepdims=True)).astype(jnp.bfloat16)
    attn_latent = jnp.einsum(
        "bhj,bjl->bhl", attn_probs, cache_latent, preferred_element_type=jnp.float32
    )
    attn_latent = attn_latent.astype(jnp.bfloat16)
    returned_flat = returned.reshape(expert_count * capacity, returned.shape[2])
    picked = jnp.take(returned_flat, slot_index.reshape(-1), axis=0).reshape(
        token_count, top_count, returned.shape[2]
    )
    moe_out = jnp.sum(gates[:, :, None] * picked.astype(jnp.float32), axis=1).astype(jnp.bfloat16)
    return (moe_out, attn_latent)


def solution(mesh):
    return jax.shard_map(
        local,
        mesh=mesh,
        in_specs=(
            P(("groups", "ep"), "tp"),
            P(("groups", "ep"), None),
            P("tp", None),
            P("ep", None, "tp"),
            P("ep", None, "tp"),
            P("ep", "tp", None),
            P(("groups", "ep"), "tp", None),
            P(("groups", "ep"), "tp", None),
            P(("groups", "ep"), None, None),
            P(("groups", "ep"), None, None),
            P(("groups", "ep")),
        ),
        out_specs=(P(("groups", "ep"), "tp"), P(("groups", "ep"), "tp", None)),
        check_vma=False,
    )
```

profile of v0, /device:TPU:514, one launch (start us, length us, event | category | flops | bytes accessed | tf_op | source)
XLA Modules:
  0.0 199.2 jit_solution(17828745028653575509)
XLA Ops:
  7.2 0.1 all-gather.3.cloned.1.call-start
  7.3 0.8 copy.21
  8.1 0.1 eq.38
  8.2 0.1 fusion.29
  8.3 0.2 reduce_window_sum.11
  8.5 0.2 select_reduce_fusion.2
  8.6 0.1 reshape.116
  8.7 0.1 convert_reduce_fusion
  8.9 1.5 fusion.7
  10.4 66.5 %all_to_all.15 = bf16[64,8,1792]{2,1,0:T(8,128)(2,1)} all-to-all(bf16[64,8,1792]{2,1,0:T(8,128)(2,1)S(1)} %fusion.7), channel_id=1, replica_groups=mesh['groups'=2,'ep'=64,'tp'=2] {'ep'}, dimensions={0} | all-to-all | bytes 3670016 | tf_op jit(solution)/shard_map/all_to_all | solution.py:61
  76.9 0.1 all-gather.3.cloned.1.call-update
  77.0 6.0 %copy.25 = bf16[3584,512]{1,0:T(8,128)(2,1)} copy(bf16[3584,512]{0,1:T(8,128)(2,1)} %bitcast.59) | data formatting | bytes 7340032 | tf_op jit(solution)/shard_map/dot_general | solution.py:68
  82.9 20.7 %all-gather.3.cloned.1.call-done = bf16[64,8,3584]{2,1,0:T(8,128)(2,1)} async-done(((bf16[64,8,1792]{2,1,0:T(8,128)(2,1)}), bf16[64,8,3584]{2,1,0:T(8,128)(2,1)}) %all-gather.3.cloned.1.call-update) | async-done | bytes 3670032 | tf_op jit(solution)/shard_map/all_gather | solution.py:62
  103.6 5.3 %fusion.3 = f32[512,512]{1,0:T(8,128)S(1)} fusion(bf16[1,3584,512]{2,1,0:T(8,128)(2,1)} %param.14, bf16[64,8,3584]{2,1,0:T(8,128)(2,1)} %all-gather.3.cloned.1.call-done), kind=kOutput, calls=%fused_computation.5 | convolution fusion | flops 1879048192 | bytes 8388608 | tf_op jit(solution)/shard_map/dot_general | solution.py:65
  109.0 2.1 %fusion.18 = bf16[512,512,1]{1,0,2:T(8,128)(2,1)S(1)} fusion(bf16[1,3584,512]{2,1,0:T(8,128)(2,1)S(1)} %copy-done.7, bf16[64,8,3584]{2,1,0:T(8,128)(2,1)S(1)} %copy-done.8, f32[512,512]{1,0:T(8,128)S(1)} %fusion.3), kind=kOutput, calls=%fused_computation.14 | convolution fusion | flops 1880621056 | bytes 8912896 | tf_op jit(solution)/shard_map/dot_general | solution.py:66
  111.2 2.1 %convolution_bitcast_fusion = f32[2,512,1792]{2,1,0:T(8,128)S(1)} fusion(bf16[512,512,1]{1,0,2:T(8,128)(2,1)S(1)} %fusion.18, bf16[2,1792,512]{2,1,0:T(8,128)(2,1)S(1)} %bitcast.57), kind=kOutput, calls=%fused_computation.2 | convolution fusion | flops 1879048192 | bytes 11534336 | tf_op jit(solution)/shard_map/dot_general | solution.py:68
  113.3 10.9 %all_to_all.16 = f32[2,512,1792]{2,1,0:T(8,128)} all-to-all(f32[2,512,1792]{2,1,0:T(8,128)S(1)} %convolution_bitcast_fusion), channel_id=1, replica_groups=mesh['groups'=2,'ep'=64,'tp'=2] {'tp'}, dimensions={0} | all-to-all | bytes 14680064 | tf_op jit(solution)/shard_map/all_to_all | solution.py:23
  124.2 5.5 %reduce_sum.77 = bf16[512,1792]{1,0:T(8,128)(2,1)} reduce(f32[2,512,1792]{2,1,0:T(8,128)} %all_to_all.16, f32[]{:T(128)} %constant.13.clone.1), dimensions={0}, to_apply=%region_6.7 | reduce | flops 917504 | bytes 9175044 | tf_op jit(solution)/shard_map/reduce_sum | solution.py:24
  129.7 13.8 %all-to-all-start.2 = ((bf16[64,8,1792]{2,1,0:T(8,128)(2,1)}), bf16[64,8,1792]{2,1,0:T(8,128)(2,1)S(1)}, u32[]{:S(2)}, u32[]{:S(2)}) async-start(bf16[64,8,1792]{2,1,0:T(8,128)(2,1)} %bitcast.58), calls=%async_computation.2 | async-start | bytes 3670016 | tf_op jit(solution)/shard_map/all_to_all | solution.py:71
  143.5 0.1 reshape.120
  143.6 0.1 fusion.35
  143.8 1.9 all-gather
  145.7 0.3 select_reduce_fusion
  146.0 0.1 iota_compare_fusion.3
  146.1 0.4 fusion.36
  146.5 0.1 fusion.27
  146.7 0.2 fusion.34
  146.8 0.1 multiply_divide_fusion
  146.9 1.0 convolution_convert_fusion.1
  147.9 42.2 %all-to-all-done.2 = bf16[64,8,1792]{2,1,0:T(8,128)(2,1)S(1)} async-done(((bf16[64,8,1792]{2,1,0:T(8,128)(2,1)}), bf16[64,8,1792]{2,1,0:T(8,128)(2,1)S(1)}, u32[]{:S(2)}, u32[]{:S(2)}) %all-to-all-start.2) | async-done | bytes 1835040 | tf_op jit(solution)/shard_map/all_to_all | solution.py:71
  190.1 0.9 gather_fusion
  191.0 1.3 multiply_reduce_fusion
  (25 shorter events, 0.1 us)
Async XLA Ops:
  7.2 138.9 %copy-start = (bf16[4,256,512]{2,1,0:T(8,128)(2,1)S(1)}, bf16[4,256,512]{2,1,0:T(8,128)(2,1)}, u32[]{:S(2)}) copy-start(bf16[4,256,512]{2,1,0:T(8,128)(2,1)} %param.19) | copy-start | bytes 3145732
  7.2 96.4 %all-gather.3.cloned.1.call-start = ((), (), s32[]{:S(2)}) async-start(), calls=%async_computation.3 | async-start | bytes 5505024 | tf_op jit(solution)/shard_map/all_gather | solution.py:62
  103.6 5.4 %copy-start.7 = (bf16[1,3584,512]{2,1,0:T(8,128)(2,1)S(1)}, bf16[1,3584,512]{2,1,0:T(8,128)(2,1)}, u32[]{:S(2)}) copy-start(bf16[1,3584,512]{2,1,0:T(8,128)(2,1)} %param.15) | copy-start | bytes 11010052
  103.6 5.4 %copy-start.8 = (bf16[64,8,3584]{2,1,0:T(8,128)(2,1)S(1)}, bf16[64,8,3584]{2,1,0:T(8,128)(2,1)}, u32[]{:S(2)}) copy-start(bf16[64,8,3584]{2,1,0:T(8,128)(2,1)} %all-gather.3.cloned.1.call-done) | copy-start | bytes 11010052
  109.0 2.2 %copy-start.1 = (bf16[3584,512]{1,0:T(8,128)(2,1)S(1)}, bf16[3584,512]{1,0:T(8,128)(2,1)}, u32[]{:S(2)}) copy-start(bf16[3584,512]{1,0:T(8,128)(2,1)} %copy.25) | copy-start | bytes 11010052
  129.6 14.0 %copy-start.2 = (bf16[1792,64]{0,1:T(8,128)(2,1)S(1)}, bf16[1792,64]{0,1:T(8,128)(2,1)}, u32[]{:S(2)}) copy-start(bf16[1792,64]{0,1:T(8,128)(2,1)} %param.13) | copy-start | bytes 688132
  129.6 14.0 %copy-start.3 = (bf16[16,1792]{1,0:T(8,128)(2,1)S(1)}, bf16[16,1792]{1,0:T(8,128)(2,1)}, u32[]{:S(2)}) copy-start(bf16[16,1792]{1,0:T(8,128)(2,1)} %param.11) | copy-start | bytes 172036
  129.6 16.4 %copy-start.9 = (s32[4]{0:T(128)S(1)}, s32[4]{0:T(128)}, u32[]{:S(2)}) copy-start(s32[4]{0:T(128)} %param.21) | copy-start | bytes 52
  129.6 16.4 %copy-start.4 = (bf16[4,32,512]{2,1,0:T(8,128)(2,1)S(1)}, bf16[4,32,512]{2,1,0:T(8,128)(2,1)}, u32[]{:S(2)}) copy-start(bf16[4,32,512]{2,1,0:T(8,128)(2,1)} %param.17) | copy-start | bytes 393220
  129.6 16.8 %copy-start.5 = (bf16[4,64,256]{2,1,0:T(8,128)(2,1)S(1)}, bf16[4,64,256]{2,1,0:T(8,128)(2,1)}, u32[]{:S(2)}) copy-start(bf16[4,64,256]{2,1,0:T(8,128)(2,1)} %param.20) | copy-start | bytes 393220
  129.6 16.9 %copy-start.6 = (bf16[4,32,64]{2,1,0:T(8,128)(2,1)S(1)}, bf16[4,32,64]{2,1,0:T(8,128)(2,1)}, u32[]{:S(2)}) copy-start(bf16[4,32,64]{2,1,0:T(8,128)(2,1)} %param.18) | copy-start | bytes 49156
  129.7 60.4 %all-to-all-start.2 = ((bf16[64,8,1792]{2,1,0:T(8,128)(2,1)}), bf16[64,8,1792]{2,1,0:T(8,128)(2,1)S(1)}, u32[]{:S(2)}, u32[]{:S(2)}) async-start(bf16[64,8,1792]{2,1,0:T(8,128)(2,1)} %bitcast.58), calls=%async_computation.2 | async-start | bytes 3670016 | tf_op jit(solution)/shard_map/all_to_all | solution.py:71
Sparse Core Ops, SparseCore 0:
  77.1 26.4 all-gather.2
where the time goes:
time: 200 us; the launch traced here: 199 us
  blocking collectives  79.3 us (40%)
  waiting for transfers between devices  62.9 us (31%)
  between operations  14.2 us (7%)
  starting transfers between devices  13.9 us (7%)
  matrix products  12.8 us (6%)
  local copies, waits for them, and re-layouts  8.03 us (4%)
  other arithmetic  8.02 us (4%)
    all_to_all x1, blocking collectives, local(): lax.all_to_all(outgoing, 'ep', split_axis=0, concat_axis=0, tiled=True)  66.5 us
    all_to_all x1, waiting for transfers between devices, local(): lax.all_to_all(summed, 'ep', split_axis=0, concat_axis=0, tiled=True)  42.2 us
    all_gather x1, waiting for transfers between devices, local(): received = lax.all_gather(received, 'tp', axis=2, tiled=True)  20.7 us
    all_to_all x1, starting transfers between devices, local(): lax.all_to_all(summed, 'ep', split_axis=0, concat_axis=0, tiled=True)  13.8 us
    all_to_all x1, blocking collectives, sum_at_owner(): lax.all_to_all(in_blocks(value, dim, devices), axis, 0, 0, tiled=True)  10.9 us
    dot_general x1, local copies, waits for them, and re-layouts, local(): jnp.dot(active, down_weight[0], preferred_element_type=jnp.float32)  5.96 us
    reduce_sum x1, other arithmetic, sum_at_owner(): return jnp.sum(tiles, axis=0)  5.46 us
    dot_general x1, matrix products, local(): jnp.dot(flat_rows, gate_weight[0], preferred_element_type=jnp.float32)  5.34 us
  transfers between devices with their start and end apart: 2, of which 2 were waited for; matrix products, arithmetic and copies ran while one was open for 4% of the time, Pallas kernels for 0%

commit v1 on v0

--- a/solution.py
+++ b/solution.py
@@ -59,7 +59,12 @@
     outgoing = jnp.dot(placing, hidden, preferred_element_type=jnp.float32).astype(jnp.bfloat16)
     outgoing = outgoing.reshape(expert_count, capacity, hidden.shape[1])
     received = lax.all_to_all(outgoing, "ep", split_axis=0, concat_axis=0, tiled=True)
-    received = lax.all_gather(received, "tp", axis=2, tiled=True)
+    rows = []
+    for _ in range(lax.axis_size("tp")):
+        rows.append(received)
+    received = jnp.concatenate(
+        lax.all_to_all(jnp.stack(rows, axis=0), axis_name="tp", split_axis=0, concat_axis=0), axis=2
+    )
     source_count, slot_count, feature_count = received.shape
     flat_rows = received.reshape(source_count * slot_count, feature_count)
     gate_part = jnp.dot(flat_rows, gate_weight[0], preferred_element_type=jnp.float32)

time: 200 us -> 182 us (0.910)
  blocking collectives: 79.3 us -> 25.5 us
  starting transfers between devices: 13.9 us -> 33.7 us
  waiting for transfers between devices: 62.9 us -> 78.5 us
  between operations: 14.2 us -> 0.81 us
  local copies, waits for them, and re-layouts: 8.03 us -> 15 us
  matrix products: 12.8 us -> 19 us
    all_to_all x1, blocking collectives: 66.5 us -> 6.7 us  [local(): lax.all_to_all(jnp.stack(rows, axis=0), axis_name='tp', split_axis=0, con...]
    all_to_all x0 -> x1, waiting for transfers between devices: none -> 36.4 us  [local(): lax.all_to_all(outgoing, 'ep', split_axis=0, concat_axis=0, tiled=True)]
    all_to_all x0 -> x1, starting transfers between devices: none -> 24.3 us  [local(): lax.all_to_all(outgoing, 'ep', split_axis=0, concat_axis=0, tiled=True)]
    all_gather x1 -> x0, waiting for transfers between devices: 20.7 us -> none  [local(): received = lax.all_gather(received, 'tp', axis=2, tiled=True)]
    dot_general x1, matrix products: 2.1 us -> 11.5 us  [local(): jnp.dot(active, down_weight[0], preferred_element_type=jnp.float32)]
    all_to_all x1, blocking collectives: 10.9 us -> 17 us  [sum_at_owner(): lax.all_to_all(in_blocks(value, dim, devices), axis, 0, 0, tiled=True)]
    all_to_all x1, starting transfers between devices: 13.8 us -> 9.46 us  [local(): lax.all_to_all(summed, 'ep', split_axis=0, concat_axis=0, tiled=True)]
    reshape x0 -> x1, local copies, waits for them, and re-layouts: none -> 3.77 us  [local(): jnp.concatenate(lax.all_to_all(jnp.stack(rows, axis=0), axis_name='tp', s...]
  transfers between devices with their start and end apart: 2 -> 2, of which waited for: 2 -> 2; matrix products, arithmetic and copies ran while one was open for 4% -> 5% of each run, Pallas kernels for 0% -> 0%
where the time goes in v1:
time: 182 us; the launch traced here: 181 us
  waiting for transfers between devices  78.5 us (43%)
  starting transfers between devices  33.7 us (19%)
  blocking collectives  25.5 us (14%)
  matrix products  19 us (10%)
  local copies, waits for them, and re-layouts  15 us (8%)
  other arithmetic  8.26 us (5%)
    all_to_all x1, waiting for transfers between devices, local(): lax.all_to_all(summed, 'ep', split_axis=0, concat_axis=0, tiled=True)  42.1 us
    all_to_all x1, waiting for transfers between devices, local(): lax.all_to_all(outgoing, 'ep', split_axis=0, concat_axis=0, tiled=True)  36.4 us
    all_to_all x1, starting transfers between devices, local(): lax.all_to_all(outgoing, 'ep', split_axis=0, concat_axis=0, tiled=True)  24.3 us
    all_to_all x1, blocking collectives, sum_at_owner(): lax.all_to_all(in_blocks(value, dim, devices), axis, 0, 0, tiled=True)  17 us
    dot_general x1, matrix products, local(): jnp.dot(active, down_weight[0], preferred_element_type=jnp.float32)  11.5 us
    all_to_all x1, starting transfers between devices, local(): lax.all_to_all(summed, 'ep', split_axis=0, concat_axis=0, tiled=True)  9.46 us
    all_to_all x1, blocking collectives, local(): lax.all_to_all(jnp.stack(rows, axis=0), axis_name='tp', split_axis=0, con...  6.7 us
    dot_general x1, local copies, waits for them, and re-layouts, local(): jnp.dot(active, down_weight[0], preferred_element_type=jnp.float32)  5.96 us
  transfers between devices with their start and end apart: 2, of which 2 were waited for; matrix products, arithmetic and copies ran while one was open for 5% of the time, Pallas kernels for 0%

profile of v1, /device:TPU:514, one launch (start us, length us, event | category | flops | bytes accessed | tf_op | source)
XLA Modules:
  0.0 180.9 jit_solution(3517207884113823425)
XLA Ops:
  0.6 0.8 copy.26
  1.5 0.1 eq.38
  1.6 0.1 fusion.24
  1.7 0.2 reduce_window_sum.11
  1.8 0.2 select_reduce_fusion.2
  2.0 0.1 reshape.116
  2.1 0.1 convert_reduce_fusion
  2.3 2.7 %fusion.5 = bf16[64,8,1792]{2,1,0:T(8,128)(2,1)} fusion(bf16[16,1792]{1,0:T(8,128)(2,1)} %param.11, s32[512,16]{0,1:T(8,128)S(1)} %convert_reduce_fusion), kind=kOutput, calls=%fused_computation.10 | convolution fusion | flops 30285824 | bytes 1925120 | tf_op jit(solution)/shard_map/dot_general | solution.py:59
  5.0 24.3 %all-to-all-start = ((bf16[64,8,1792]{2,1,0:T(8,128)(2,1)}), bf16[64,8,1792]{2,1,0:T(8,128)(2,1)S(1)}, u32[]{:S(2)}, u32[]{:S(2)}) async-start(bf16[64,8,1792]{2,1,0:T(8,128)(2,1)} %fusion.5), calls=%async_computation | async-start | bytes 3670016 | tf_op jit(solution)/shard_map/all_to_all | solution.py:61
  29.3 6.0 %copy.31 = bf16[3584,512]{1,0:T(8,128)(2,1)} copy(bf16[3584,512]{0,1:T(8,128)(2,1)} %bitcast.61) | data formatting | bytes 7340032 | tf_op jit(solution)/shard_map/dot_general | solution.py:73
  35.3 36.4 %all-to-all-done = bf16[64,8,1792]{2,1,0:T(8,128)(2,1)S(1)} async-done(((bf16[64,8,1792]{2,1,0:T(8,128)(2,1)}), bf16[64,8,1792]{2,1,0:T(8,128)(2,1)S(1)}, u32[]{:S(2)}, u32[]{:S(2)}) %all-to-all-start) | async-done | bytes 1835040 | tf_op jit(solution)/shard_map/all_to_all | solution.py:61
  71.7 0.3 pad_maximum_fusion
  72.0 6.7 %all_to_all.20 = bf16[2,64,8,1792]{3,2,1,0:T(8,128)(2,1)S(1)} all-to-all(bf16[2,64,8,1792]{3,2,1,0:T(8,128)(2,1)S(1)} %pad_maximum_fusion), channel_id=1, replica_groups=mesh['groups'=2,'ep'=64,'tp'=2] {'tp'}, dimensions={0} | all-to-all | bytes 7340032 | tf_op jit(solution)/shard_map/all_to_all | solution.py:66
  78.7 3.8 %copy.34 = bf16[64,8,2,1792]{3,2,1,0:T(2,128)(2,1)S(1)} copy(bf16[64,8,2,1792]{3,1,0,2:T(8,128)(2,1)S(1)} %bitcast.58) | data formatting | bytes 7340032 | tf_op jit(solution)/shard_map/reshape | solution.py:65
  82.5 0.6 copy.32
  83.1 2.6 %copy-done.7 = bf16[1,3584,512]{2,1,0:T(8,128)(2,1)S(1)} copy-done((bf16[1,3584,512]{2,1,0:T(8,128)(2,1)S(1)}, bf16[1,3584,512]{2,1,0:T(8,128)(2,1)}, u32[]{:S(2)}) %copy-start.7) | copy-done | bytes 3670040
  85.8 3.1 %fusion.3 = f32[512,512]{1,0:T(8,128)} fusion(bf16[512,3584]{1,0:T(8,128)(2,1)S(1)} %bitcast.63, bf16[1,3584,512]{2,1,0:T(8,128)(2,1)S(1)} %copy-done.7), kind=kOutput, calls=%fused_computation.6 | convolution fusion | flops 1879048192 | bytes 8388608 | tf_op jit(solution)/shard_map/dot_general | solution.py:70
  88.8 11.5 %convolution_bitcast_fusion = f32[2,512,1792]{2,1,0:T(8,128)} fusion(bf16[2,1792,512]{2,1,0:T(8,128)(2,1)} %bitcast.62, bf16[512,3584]{1,0:T(8,128)(2,1)} %bitcast.64, bf16[1,3584,512]{2,1,0:T(8,128)(2,1)} %param.15, f32[512,512]{1,0:T(8,128)} %fusion.3), kind=kOutput, calls=%fused_computation.2 | convolution fusion | flops 3759669248 | bytes 19398656 | tf_op jit(solution)/shard_map/dot_general | solution.py:73
  100.3 17.0 %all_to_all.21 = f32[2,512,1792]{2,1,0:T(8,128)} all-to-all(f32[2,512,1792]{2,1,0:T(8,128)} %convolution_bitcast_fusion), channel_id=1, replica_groups=mesh['groups'=2,'ep'=64,'tp'=2] {'tp'}, dimensions={0} | all-to-all | bytes 14680064 | tf_op jit(solution)/shard_map/all_to_all | solution.py:23
  117.3 5.4 %reduce_sum.77 = bf16[512,1792]{1,0:T(8,128)(2,1)} reduce(f32[2,512,1792]{2,1,0:T(8,128)} %all_to_all.21, f32[]{:T(128)} %constant.13.clone.1), dimensions={0}, to_apply=%region_6.7 | reduce | flops 917504 | bytes 9175044 | tf_op jit(solution)/shard_map/reduce_sum | solution.py:24
  122.7 9.5 %all-to-all-start.3 = ((bf16[64,8,1792]{2,1,0:T(8,128)(2,1)}), bf16[64,8,1792]{2,1,0:T(8,128)(2,1)S(1)}, u32[]{:S(2)}, u32[]{:S(2)}) async-start(bf16[64,8,1792]{2,1,0:T(8,128)(2,1)} %bitcast.59), calls=%async_computation.3 | async-start | bytes 3670016 | tf_op jit(solution)/shard_map/all_to_all | solution.py:76
  132.2 0.1 reshape.120
  132.3 0.1 fusion.31
  132.4 1.9 %all-gather = f32[32,64]{1,0:T(8,128)S(1)} all-gather(f32[16,64]{1,0:T(8,128)S(1)} %fusion.31), channel_id=2, replica_groups=mesh['groups'=2,'ep'=64,'tp'=2] {'tp'}, dimensions={0}, use_global_device_ids=true | all-gather | bytes 12288 | tf_op jit(solution)/shard_map/all_gather | solution.py:11
  134.3 0.3 select_reduce_fusion
  134.7 0.4 fusion.32
  135.1 0.2 fusion.19
  135.3 0.2 fusion.30
  135.6 1.0 convolution_convert_fusion.1
  136.6 42.1 %all-to-all-done.3 = bf16[64,8,1792]{2,1,0:T(8,128)(2,1)S(1)} async-done(((bf16[64,8,1792]{2,1,0:T(8,128)(2,1)}), bf16[64,8,1792]{2,1,0:T(8,128)(2,1)S(1)}, u32[]{:S(2)}, u32[]{:S(2)}) %all-to-all-start.3) | async-done | bytes 1835040 | tf_op jit(solution)/shard_map/all_to_all | solution.py:76
  178.7 0.9 gather_fusion
  179.6 1.3 multiply_reduce_fusion
  (24 shorter events, 0.3 us)
Async XLA Ops:
  0.6 134.1 %copy-start = (bf16[4,256,512]{2,1,0:T(8,128)(2,1)S(1)}, bf16[4,256,512]{2,1,0:T(8,128)(2,1)}, u32[]{:S(2)}) copy-start(bf16[4,256,512]{2,1,0:T(8,128)(2,1)} %param.19) | copy-start | bytes 3145732
  5.0 66.7 %all-to-all-start = ((bf16[64,8,1792]{2,1,0:T(8,128)(2,1)}), bf16[64,8,1792]{2,1,0:T(8,128)(2,1)S(1)}, u32[]{:S(2)}, u32[]{:S(2)}) async-start(bf16[64,8,1792]{2,1,0:T(8,128)(2,1)} %fusion.5), calls=%async_computation | async-start | bytes 3670016 | tf_op jit(solution)/shard_map/all_to_all | solution.py:61
  82.5 3.2 %copy-start.7 = (bf16[1,3584,512]{2,1,0:T(8,128)(2,1)S(1)}, bf16[1,3584,512]{2,1,0:T(8,128)(2,1)}, u32[]{:S(2)}) copy-start(bf16[1,3584,512]{2,1,0:T(8,128)(2,1)} %param.14) | copy-start | bytes 11010052
  83.1 5.7 %copy-start.1 = (bf16[64,8,2,1792]{3,1,2,0:T(8,128)(2,1)}, bf16[64,8,2,1792]{3,1,2,0:T(8,128)(2,1)S(1)}, u32[]{:S(2)}) copy-start(bf16[64,8,2,1792]{3,1,2,0:T(8,128)(2,1)S(1)} %copy.32) | copy-start | bytes 11010052
  122.7 9.6 %copy-start.2 = (bf16[1792,64]{0,1:T(8,128)(2,1)S(1)}, bf16[1792,64]{0,1:T(8,128)(2,1)}, u32[]{:S(2)}) copy-start(bf16[1792,64]{0,1:T(8,128)(2,1)} %param.13) | copy-start | bytes 688132
  122.7 9.6 %copy-start.3 = (bf16[16,1792]{1,0:T(8,128)(2,1)S(1)}, bf16[16,1792]{1,0:T(8,128)(2,1)}, u32[]{:S(2)}) copy-start(bf16[16,1792]{1,0:T(8,128)(2,1)} %param.11) | copy-start | bytes 172036
  122.7 12.0 %copy-start.8 = (s32[4]{0:T(128)S(1)}, s32[4]{0:T(128)}, u32[]{:S(2)}) copy-start(s32[4]{0:T(128)} %param.21) | copy-start | bytes 52
  122.7 12.1 %copy-start.4 = (bf16[4,32,512]{2,1,0:T(8,128)(2,1)S(1)}, bf16[4,32,512]{2,1,0:T(8,128)(2,1)}, u32[]{:S(2)}) copy-start(bf16[4,32,512]{2,1,0:T(8,128)(2,1)} %param.17) | copy-start | bytes 393220
  122.7 12.5 %copy-start.5 = (bf16[4,64,256]{2,1,0:T(8,128)(2,1)S(1)}, bf16[4,64,256]{2,1,0:T(8,128)(2,1)}, u32[]{:S(2)}) copy-start(bf16[4,64,256]{2,1,0:T(8,128)(2,1)} %param.20) | copy-start | bytes 393220
  122.7 12.5 %copy-start.6 = (bf16[4,32,64]{2,1,0:T(8,128)(2,1)S(1)}, bf16[4,32,64]{2,1,0:T(8,128)(2,1)}, u32[]{:S(2)}) copy-start(bf16[4,32,64]{2,1,0:T(8,128)(2,1)} %param.18) | copy-start | bytes 49156
  122.7 56.0 %all-to-all-start.3 = ((bf16[64,8,1792]{2,1,0:T(8,128)(2,1)}), bf16[64,8,1792]{2,1,0:T(8,128)(2,1)S(1)}, u32[]{:S(2)}, u32[]{:S(2)}) async-start(bf16[64,8,1792]{2,1,0:T(8,128)(2,1)} %bitcast.59), calls=%async_computation.3 | async-start | bytes 3670016 | tf_op jit(solution)/shard_map/all_to_all | solution.py:76
